TPU v7x, 32 devices: a whole 2x2x4 slice. The times are simulated.
32 devices in a mesh: slab: 4 (over x, core), patch: 8 (over z, y).
Axes of the slice: x: 2, y: 2, z: 4, core: 2. Of those that a mesh axis runs over, the one named last changes fastest.
Arguments:
- right_side: float32 [4, 8, 256, 768], P('slab', 'patch'), may hold values from -6 to 6
- inverse_factor: bfloat16 [4, 8, 768, 768], P('slab', 'patch'), may hold values from -0.12990381 to 1.5, as said below
- forward_trace: bfloat16 [4, 8, 128, 768], P('slab', 'patch'), may hold values from -0.375 to 0.375
- backward_trace: bfloat16 [4, 8, 128, 768], P('slab', 'patch'), may hold values from -0.375 to 0.375
- margin: int32 [4, 8], P('slab', 'patch'), may hold values from 1 to 256, as said below
Outputs:
- correction: float32 [4, 8, 256, 768], P('slab', 'patch')
Inputs may be any that keep to these rules, and one draw needn't show every extreme that they name: `inverse_factor`: lower triangular: zero above the diagonal, positive on it. margin[s, q] counts the last unknowns of patch q that are the first unknowns of patch q + 1 (of patch 0 for q = 7). In every slab some pair shares exactly 256.
All inputs are finite; a program needn't handle non-finite values.
Results may differ from a plain program's by a relative error of at most 0.035.
Values may be sent and summed in bfloat16 or wider, within the bound.
A program may use at most 64 MiB of HBM per device.

v0:
```python
import functools

import jax
import jax.numpy as jnp
from jax import lax
from jax.experimental import pallas as pl
from jax.experimental.pallas import tpu as pltpu
from jax.sharding import PartitionSpec as P

KMAX = 256
BF = jnp.bfloat16
F32 = jnp.float32
MESH = pl.DeviceIdType.MESH


def nt(a, b):
    return lax.dot_general(a, b, (((1,), (1,)), ((), ())), preferred_element_type=F32)


def nn(a, b):
    return lax.dot_general(a, b, (((1,), (0,)), ((), ())), preferred_element_type=F32)


def tn(a, b):
    return lax.dot_general(a, b, (((0,), (0,)), ((), ())), preferred_element_type=F32)


def halfway(x, fac, m):
    return jnp.concatenate(
        [nt(x[:, : i + KMAX], fac[i : i + KMAX, : i + KMAX]).astype(BF) for i in range(0, m, KMAX)],
        axis=1,
    )


def solve(x, fac, m):
    half = halfway(x, fac, m)
    return [nn(half[:, k:], fac[k:, k : k + KMAX]) for k in range(0, m, KMAX)]


def finish(half_ref, l_ref, out_ref, held, sem):
    m = half_ref.shape[1]
    copies = []
    for n, k in enumerate(range(0, m, KMAX)):
        held[n] = nn(half_ref[:, k:], l_ref[0, 0, k:, k : k + KMAX])
        copies.append(pltpu.make_async_copy(held.at[n], out_ref.at[0, 0, :, k : k + KMAX], sem.at[n]))
        copies[-1].start()
    for c in copies:
        c.wait()


def kernel(
    slabs, patches, parts,
    r_hbm, l_hbm, f_hbm, b_hbm, margin_ref, out_ref,
    r_v, fac, maps,
    tail_s, head_s, zt_s, zh_s, d_s, u_s,
    tail_r, head_r, zt_r, zh_r, d_r, u_r,
    adj, acc, gt, opd, opu, place, zr,
    load_sem, send_sem, recv_sem,
):
    s = lax.axis_index("slab")
    q = lax.axis_index("patch")
    left = lax.rem(q + patches - 1, patches)
    right = lax.rem(q + 1, patches)
    around = (left, right, q)
    m = fac.shape[-1]
    face = f_hbm.shape[-2]
    cols = r_v.shape[0]
    step = cols // parts
    first_slab, last_slab = s == 0, s == slabs - 1
    inner_low, inner_high = s > 0, s < slabs - 1

    loads = [
        pltpu.make_async_copy(r_hbm.at[0, 0], r_v, load_sem.at[0]),
        pltpu.make_async_copy(l_hbm.at[0, 0], fac, load_sem.at[1]),
        pltpu.make_async_copy(f_hbm.at[0, 0], maps.at[:face], load_sem.at[2]),
        pltpu.make_async_copy(b_hbm.at[0, 0], maps.at[face:], load_sem.at[3]),
    ]
    for c in loads:
        c.start()

    barrier = pltpu.get_barrier_semaphore()

    def greet(slab, patch):
        pl.semaphore_signal(barrier, inc=1, device_id=(slab, patch), device_id_type=MESH)

    greet(s, left)
    greet(s, right)

    @pl.when(inner_low)
    def _():
        for p in around:
            greet(s - 1, p)

    @pl.when(inner_high)
    def _():
        for p in around:
            greet(s + 1, p)

    slot = [0]

    def send(src, dst, slab, patch):
        n = slot[0]
        slot[0] += 1
        return pltpu.make_async_remote_copy(
            src_ref=src, dst_ref=dst, send_sem=send_sem.at[n], recv_sem=recv_sem.at[n],
            device_id=(slab, patch), device_id_type=MESH,
        )

    rows = [pl.ds(c * step, step) for c in range(parts)]
    tail_c = [send(tail_s.at[w], tail_r.at[w], s, right) for w in rows]
    head_c = [send(head_s.at[w], head_r.at[w], s, left) for w in rows]
    low_rows, high_rows = pl.ds(0, face), pl.ds(face, face)
    zd_c = [send(zt_s.at[low_rows], zt_r.at[low_rows], s, right), send(zh_s.at[low_rows], zh_r.at[low_rows], s, left)]
    zu_c = [send(zt_s.at[high_rows], zt_r.at[high_rows], s, right), send(zh_s.at[high_rows], zh_r.at[high_rows], s, left)]
    targets = ((2, left), (1, right), (0, q))
    down_c = [[send(d_s.at[w], d_r.at[j, w], s + 1, p) for j, p in targets] for w in rows]
    up_c = [[send(u_s.at[w], u_r.at[j, w], s - 1, p) for j, p in targets] for w in rows]

    count = margin_ref[0, 0]
    row = lax.broadcasted_iota(jnp.int32, (KMAX, KMAX), 0)
    col = lax.broadcasted_iota(jnp.int32, (KMAX, KMAX), 1)
    hit = (row == KMAX - count + col) & (col < count)
    place[...] = jnp.where(hit, 1.0, 0.0).astype(BF)

    loads[0].wait()
    loads[1].wait()
    first = solve(r_v[...].astype(BF), fac, m)
    tail_s[...] = nn(first[-1].astype(BF), place[...]).astype(BF)
    head_s[...] = first[0].astype(BF)

    pl.semaphore_wait(barrier, 2 + 3 * inner_low.astype(jnp.int32) + 3 * inner_high.astype(jnp.int32))

    for a, b in zip(tail_c, head_c):
        a.start()
        b.start()

    loads[2].wait()
    loads[3].wait()
    for k, part in enumerate(solve(maps[...], fac, m)):
        gt[:, k * KMAX : (k + 1) * KMAX] = part.astype(BF)

    low = fac[:, :face]
    high = fac[m - face :, m - face :]
    k_tail = jnp.concatenate(
        [tn(low[m - KMAX :], fac[m - KMAX :, m - KMAX :]), tn(high, fac[m - face :, m - KMAX :])], axis=0
    )
    k_head = jnp.concatenate([tn(low, fac[:, :KMAX]), tn(high, fac[m - face :, :KMAX])], axis=0)
    zt_s[...] = nn(k_tail.astype(BF), place[...]).astype(BF)
    zh_s[...] = k_head.astype(BF)

    @pl.when(inner_low)
    def _():
        for c in zd_c:
            c.start()

    @pl.when(inner_low & inner_high)
    def _():
        for c in zu_c:
            c.start()

    def send_down(c):
        w = rows[c]
        d_s[w] = acc[w, :face].astype(BF)
        for x in down_c[c]:
            x.start()

    def send_up(c):
        w = rows[c]
        u_s[w] = acc[w, face:].astype(BF)
        for x in up_c[c]:
            x.start()

    for c, w in enumerate(rows):
        tail_c[c].wait_recv()
        head_c[c].wait_recv()
        adj[w, :] = r_v[w, :]
        adj[w, :KMAX] = adj[w, :KMAX] - 0.5 * tail_r[w].astype(F32)
        adj[w, m - KMAX :] = adj[w, m - KMAX :] - 0.5 * nt(head_r[w], place[...])
        acc[w, :face] = nt(adj[w, :].astype(BF), gt[:face])

        @pl.when(first_slab)
        def _():
            send_down(c)

    @pl.when(first_slab)
    def _():
        for c in zu_c:
            c.start()

    acc[:, face:] = nt(adj[...].astype(BF), gt[face:])

    @pl.when(inner_low)
    def _():
        for c in zd_c:
            c.wait_recv()
        zr[low_rows] = nt(zh_r[low_rows], place[...]).astype(BF)
        opd[:face, :] = (-gt[:, :face].astype(F32)).T.astype(BF)
        opd[face : 2 * face, :] = (0.5 * nt(zt_r[low_rows], gt[:, :KMAX])).astype(BF)
        opd[2 * face :, :] = (0.5 * nt(zr[low_rows], gt[:, m - KMAX :])).astype(BF)

    def make_up():
        for c in zu_c:
            c.wait_recv()
        zr[high_rows] = nt(zh_r[high_rows], place[...]).astype(BF)

        @pl.when(inner_low)
        def _():
            opu[:face, :] = (-gt[face:, m - face :].astype(F32)).T.astype(BF)
            opu[face : 2 * face, :] = (0.5 * nt(zt_r[high_rows], gt[face:, :KMAX])).astype(BF)
            opu[2 * face :, :] = (0.5 * nt(zr[high_rows], gt[face:, m - KMAX :])).astype(BF)

    def beside(ref, w):
        return jnp.concatenate([ref[0, w], ref[1, w], ref[2, w]], axis=1)

    @pl.when(inner_low)
    def _():
        for c, w in enumerate(rows):
            for x in down_c[c]:
                x.wait_recv()

            @pl.when(inner_high)
            def _():
                acc[w, :face] += nn(beside(d_r, w), opd[:, :face])
                send_down(c)

            @pl.when(last_slab)
            def _():
                acc[w, face:] += nn(beside(d_r, w), opd[:, face:])
                send_up(c)

        @pl.when(inner_high)
        def _():
            every = pl.ds(0, cols)
            acc[:, face:] += nn(beside(d_r, every), opd[:, face:])

        adj[:, :face] = adj[:, :face] - d_r[0].astype(F32)
        adj[:, :KMAX] = adj[:, :KMAX] + 0.5 * nn(d_r[1], zt_r[low_rows])
        adj[:, m - KMAX :] = adj[:, m - KMAX :] + 0.5 * nn(d_r[2], zr[low_rows])

    @pl.when(inner_high)
    def _():
        make_up()
        for c, w in enumerate(rows):
            for x in up_c[c]:
                x.wait_recv()

            @pl.when(inner_low)
            def _():
                acc[w, face:] += nn(beside(u_r, w), opu[...])
                send_up(c)

            adj[w, m - face :] = adj[w, m - face :] - u_r[0, w].astype(F32)
            adj[w, :KMAX] = adj[w, :KMAX] + 0.5 * nn(u_r[1, w], zt_r[high_rows])
            adj[w, m - KMAX :] = adj[w, m - KMAX :] + 0.5 * nn(u_r[2, w], zr[high_rows])

    out_ref[...] = halfway(adj[...].astype(BF), fac, m)

    for c in tail_c + head_c:
        c.wait_send()

    @pl.when(inner_low)
    def _():
        for c in zd_c:
            c.wait_send()
        for group in up_c:
            for x in group:
                x.wait_send()

    @pl.when(inner_high)
    def _():
        for c in zu_c:
            c.wait_send()
        for group in down_c:
            for x in group:
                x.wait_send()


def on_device(slabs, patches, right_side, inverse_factor, forward_trace, backward_trace, margin):
    cols, m = right_side.shape[2:]
    face = forward_trace.shape[2]
    parts = 4
    copies = 2 * parts + 4 + 6 * parts
    wide = pltpu.VMEM((cols, KMAX), BF)
    square = pltpu.VMEM((2 * face, KMAX), BF)
    thin = pltpu.VMEM((cols, face), BF)
    three = pltpu.VMEM((3, cols, face), BF)
    hbm = pl.BlockSpec(memory_space=pltpu.HBM)
    half = pl.pallas_call(
        functools.partial(kernel, slabs, patches, parts),
        out_shape=jax.ShapeDtypeStruct((cols, m), BF),
        in_specs=[hbm, hbm, hbm, hbm, pl.BlockSpec(memory_space=pltpu.SMEM)],
        out_specs=pl.BlockSpec(memory_space=pltpu.VMEM),
        scratch_shapes=[
            pltpu.VMEM((cols, m), F32),
            pltpu.VMEM((m, m), BF),
            pltpu.VMEM((2 * face, m), BF),
            wide, wide, square, square, thin, thin,
            wide, wide, square, square, three, three,
            pltpu.VMEM((cols, m), F32),
            pltpu.VMEM((cols, 2 * face), F32),
            pltpu.VMEM((2 * face, m), BF),
            pltpu.VMEM((3 * face, 2 * face), BF),
            pltpu.VMEM((3 * face, face), BF),
            pltpu.VMEM((KMAX, KMAX), BF),
            square,
            pltpu.SemaphoreType.DMA((4,)),
            pltpu.SemaphoreType.DMA((copies,)),
            pltpu.SemaphoreType.DMA((copies,)),
        ],
        compiler_params=pltpu.CompilerParams(collective_id=0, has_side_effects=True),
        name="sweeps",
    )(right_side, inverse_factor, forward_trace, backward_trace, margin)
    return pl.pallas_call(
        finish,
        out_shape=jax.ShapeDtypeStruct(right_side.shape, F32),
        in_specs=[pl.BlockSpec(memory_space=pltpu.VMEM)] * 2,
        out_specs=hbm,
        scratch_shapes=[pltpu.VMEM((m // KMAX, cols, KMAX), F32), pltpu.SemaphoreType.DMA((m // KMAX,))],
        compiler_params=pltpu.CompilerParams(vmem_limit_bytes=16 << 20),
        name="finish",
    )(half, inverse_factor)


def solution(mesh):
    four = P("slab", "patch", None, None)
    return jax.shard_map(
        functools.partial(on_device, mesh.shape["slab"], mesh.shape["patch"]),
        mesh=mesh,
        in_specs=(four, four, four, four, P("slab", "patch")),
        out_specs=four,
        check_vma=False,
    )
```

profile of v0, /device:TPU:0, one launch (start us, length us, event | category | flops | bytes accessed | tf_op | source)
XLA Modules:
  0.0 43.2 jit_solution(7206255783285314177)
XLA Ops:
  0.7 0.0 copy-start
  0.7 40.3 %sweeps.1.half_ref = bf16[256,768]{1,0:T(8,128)(2,1)} custom-call(f32[1,1,256,768]{3,2,1,0:T(8,128)} %r_hbm.1, bf16[1,1,768,768]{3,2,1,0:T(8,128)(2,1)} %l_ref.1, bf16[1,1,128,768]{3,2,1,0:T(8,128)(2,1)} %f_hbm.1, bf16[1,1,128,768]{3,2,1,0:T(8,128)(2,1)} %b_hbm.1, s32[1,1]{1,0:T(1,128)S(6)} %copy.6.margin_ref), custom_call_target="tpu_custom_call" | custom-call | tf_op jit(solution)/shard_map/sweeps/pallas_call | solution.py:288
  40.9 0.0 copy-done
  40.9 0.0 copy-start.1
  40.9 1.0 %copy-done.1 = bf16[256,768]{1,0:T(8,128)(2,1)S(1)} copy-done((bf16[256,768]{1,0:T(8,128)(2,1)S(1)}, bf16[256,768]{1,0:T(8,128)(2,1)}, u32[]{:S(2)}) %copy-start.1) | copy-done | bytes 393240
  41.9 1.3 %finish.1 = f32[1,1,256,768]{3,2,1,0:T(8,128)} custom-call(bf16[256,768]{1,0:T(8,128)(2,1)S(1)} %copy-done.1, bf16[1,1,768,768]{3,2,1,0:T(8,128)(2,1)S(1)} %copy-done), custom_call_target="tpu_custom_call" | custom-call | tf_op jit(solution)/shard_map/finish/pallas_call | solution.py:313
Async XLA Ops:
  0.7 40.3 %copy-start = (bf16[1,1,768,768]{3,2,1,0:T(8,128)(2,1)S(1)}, bf16[1,1,768,768]{3,2,1,0:T(8,128)(2,1)}, u32[]{:S(2)}) copy-start(bf16[1,1,768,768]{3,2,1,0:T(8,128)(2,1)} %l_ref.1) | copy-start | bytes 3538948
  40.9 1.0 %copy-start.1 = (bf16[256,768]{1,0:T(8,128)(2,1)S(1)}, bf16[256,768]{1,0:T(8,128)(2,1)}, u32[]{:S(2)}) copy-start(bf16[256,768]{1,0:T(8,128)(2,1)} %sweeps.1.half_ref) | copy-start | bytes 1179652
where the time goes:
time: 43.4 us; the launch traced here: 43.2 us
  Pallas kernels  41.5 us (96%)
  local copies, waits for them, and re-layouts  0.99 us (2%)
  between operations  0.68 us (2%)
    pallas_call x1, Pallas kernels, on_device(): pl.pallas_call(functools.partial(kernel, slabs, patches, parts), out_shap...  40.3 us
    pallas_call x1, Pallas kernels, on_device(): pl.pallas_call(finish, out_shape=jax.ShapeDtypeStruct(right_side.shape, F...  1.27 us
    unnamed x4, local copies, waits for them, and re-layouts  0.99 us

commit v1 on v0

--- a/solution.py
+++ b/solution.py
@@ -287,7 +287,7 @@
     hbm = pl.BlockSpec(memory_space=pltpu.HBM)
     half = pl.pallas_call(
         functools.partial(kernel, slabs, patches, parts),
-        out_shape=jax.ShapeDtypeStruct((cols, m), BF),
+        out_shape=pltpu.VMEM((cols, m), BF),
         in_specs=[hbm, hbm, hbm, hbm, pl.BlockSpec(memory_space=pltpu.SMEM)],
         out_specs=pl.BlockSpec(memory_space=pltpu.VMEM),
         scratch_shapes=[

time: 43.4 us -> 41.6 us (0.959)
  local copies, waits for them, and re-layouts: 0.99 us -> 0.01 us
  Pallas kernels: 41.5 us -> 40.8 us
    unnamed x4 -> x2, local copies, waits for them, and re-layouts: 0.99 us -> 0.01 us
    pallas_call x1, Pallas kernels: 40.3 us -> 39.5 us  [on_device(): pl.pallas_call(functools.partial(kernel, slabs, patches, parts), out_shap...]
where the time goes in v1:
time: 41.6 us; the launch traced here: 41.5 us
  Pallas kernels  40.8 us (98%)
  between operations  0.68 us (2%)
    pallas_call x1, Pallas kernels, on_device(): pl.pallas_call(functools.partial(kernel, slabs, patches, parts), out_shap...  39.5 us
    pallas_call x1, Pallas kernels, on_device(): pl.pallas_call(finish, out_shape=jax.ShapeDtypeStruct(right_side.shape, F...  1.27 us

profile of v1, /device:TPU:0, one launch (start us, length us, event | category | flops | bytes accessed | tf_op | source)
XLA Modules:
  0.0 41.5 jit_solution(7477434949128139825)
XLA Ops:
  0.7 0.0 copy-start
  0.7 39.5 %sweeps.1.half_ref = bf16[256,768]{1,0:T(8,128)(2,1)S(1)} custom-call(f32[1,1,256,768]{3,2,1,0:T(8,128)} %r_hbm.1, bf16[1,1,768,768]{3,2,1,0:T(8,128)(2,1)} %l_ref.1, bf16[1,1,128,768]{3,2,1,0:T(8,128)(2,1)} %f_hbm.1, bf16[1,1,128,768]{3,2,1,0:T(8,128)(2,1)} %b_hbm.1, s32[1,1]{1,0:T(1,128)S(6)} %copy.6.margin_ref), custom_call_target="tpu_custom_call" | custom-call | tf_op jit(solution)/shard_map/sweeps/pallas_call | solution.py:288
  40.2 0.0 copy-done
  40.2 1.3 %finish.1 = f32[1,1,256,768]{3,2,1,0:T(8,128)} custom-call(bf16[256,768]{1,0:T(8,128)(2,1)S(1)} %sweeps.1.half_ref, bf16[1,1,768,768]{3,2,1,0:T(8,128)(2,1)S(1)} %copy-done), custom_call_target="tpu_custom_call" | custom-call | tf_op jit(solution)/shard_map/finish/pallas_call | solution.py:313
Async XLA Ops:
  0.7 39.5 %copy-start = (bf16[1,1,768,768]{3,2,1,0:T(8,128)(2,1)S(1)}, bf16[1,1,768,768]{3,2,1,0:T(8,128)(2,1)}, u32[]{:S(2)}) copy-start(bf16[1,1,768,768]{3,2,1,0:T(8,128)(2,1)} %l_ref.1) | copy-start | bytes 3538948

commit v2 on v1

v2 whole, which is shorter than its diff:
```python
import functools

import jax
import jax.numpy as jnp
from jax import lax
from jax.experimental import pallas as pl
from jax.experimental.pallas import tpu as pltpu
from jax.sharding import PartitionSpec as P

KMAX = 256
BF = jnp.bfloat16
F32 = jnp.float32
MESH = pl.DeviceIdType.MESH


def nt(a, b):
    return lax.dot_general(a, b, (((1,), (1,)), ((), ())), preferred_element_type=F32)


def nn(a, b):
    return lax.dot_general(a, b, (((1,), (0,)), ((), ())), preferred_element_type=F32)


def tn(a, b):
    return lax.dot_general(a, b, (((0,), (0,)), ((), ())), preferred_element_type=F32)


def halfway(x, fac, m):
    return jnp.concatenate(
        [nt(x[:, : i + KMAX], fac[i : i + KMAX, : i + KMAX]).astype(BF) for i in range(0, m, KMAX)],
        axis=1,
    )


def solve(x, fac, m):
    half = halfway(x, fac, m)
    return [nn(half[:, k:], fac[k:, k : k + KMAX]) for k in range(0, m, KMAX)]


def finish(half_ref, l_ref, out_ref, held, sem):
    m = half_ref.shape[1]
    copies = []
    for n, k in enumerate(range(0, m, KMAX)):
        held[n] = nn(half_ref[:, k:], l_ref[0, 0, k:, k : k + KMAX])
        copies.append(pltpu.make_async_copy(held.at[n], out_ref.at[0, 0, :, k : k + KMAX], sem.at[n]))
        copies[-1].start()
    for c in copies:
        c.wait()


FAR_LEFT, FAR_RIGHT, LEFT, RIGHT, OWN = range(5)


class Names:
    def __init__(self):
        self.count = 0

    def take(self):
        self.count += 1
        return self.count - 1


def kernel(
    slabs, patches,
    r_hbm, l_hbm, f_hbm, b_hbm, margin_ref, out_ref,
    r_v, fac, maps,
    tail_s, head_s, zt_s, zh_s, d_s, a_s, b_s, t_s, v_s, w_s,
    tail_r, head_r, zt_r, zh_r, d_home, u_home,
    a_h, b_h, t_h, w_h, d_h, u_h, u0_s,
    adj, gt, place, zr,
    load_sem, send_sem, near_sem, home_sem, fed_sem, ring_sem, turn_sem,
):
    s = lax.axis_index("slab")
    q = lax.axis_index("patch")
    left = lax.rem(q + patches - 1, patches)
    right = lax.rem(q + 1, patches)
    m = fac.shape[-1]
    face = f_hbm.shape[-2]
    cols = r_v.shape[0]
    hosts = range(1, slabs, 2)
    wide = cols // len(hosts)
    inner_low, inner_high = s > 0, s < slabs - 1
    first_slab = s == 0
    pair = s + 1 - 2 * lax.rem(s, 2)
    host = lax.rem(s, 2) == 1
    next_left = lax.rem(q + patches - 2, patches)
    next_right = lax.rem(q + 2, patches)

    loads = [
        pltpu.make_async_copy(l_hbm.at[0, 0], fac, load_sem.at[1]),
        pltpu.make_async_copy(r_hbm.at[0, 0], r_v, load_sem.at[0]),
        pltpu.make_async_copy(f_hbm.at[0, 0], maps.at[:face], load_sem.at[2]),
        pltpu.make_async_copy(b_hbm.at[0, 0], maps.at[face:], load_sem.at[3]),
    ]
    for c in loads:
        c.start()

    barrier = pltpu.get_barrier_semaphore()

    def greet(slab, patch):
        pl.semaphore_signal(barrier, inc=1, device_id=(slab, patch), device_id_type=MESH)

    greet(s, left)
    greet(s, right)
    greet(pair, q)

    @pl.when(first_slab)
    def _():
        for h in hosts:
            for p in (left, q, right):
                greet(h, p)

    @pl.when(inner_low)
    def _():
        for h in hosts:
            @pl.when(s != h)
            def _():
                greet(h, q)

                @pl.when(host)
                def _():
                    greet(h, left)
                    greet(h, right)

    @pl.when(host)
    def _():
        greet(s, next_left)
        greet(s, next_right)
        for p in (left, q, right):
            greet(0, p)
        for t in range(1, slabs):
            @pl.when(s != t)
            def _():
                greet(t, q)

    here = host.astype(jnp.int32)
    greeted = (
        3
        + first_slab.astype(jnp.int32) * (3 * len(hosts))
        + inner_low.astype(jnp.int32) * len(hosts)
        + here * (2 * (len(hosts) - 1) + slabs + 2)
    )

    names = Names()

    def send(src, dst, recv, slab, patch):
        return pltpu.make_async_remote_copy(
            src_ref=src, dst_ref=dst, send_sem=send_sem.at[names.take()], recv_sem=recv,
            device_id=(slab, patch), device_id_type=MESH,
        )

    class Post:
        def __init__(self, here, src, dst, recv, slab, patch):
            self.here = here
            self.local = pltpu.make_async_copy(src, dst, recv)
            self.remote = send(src, dst, recv, slab, patch)

        def start(self):
            @pl.when(self.here)
            def _():
                self.local.start()

            @pl.when(~self.here)
            def _():
                self.remote.start()

        def wait_send(self):
            @pl.when(~self.here)
            def _():
                self.remote.wait_send()

    def arrived(dst, recv):
        pltpu.make_async_copy(dst, dst, recv).wait()

    part = [pl.ds(g * wide, wide) for g in range(len(hosts))]
    low_rows, high_rows = pl.ds(0, face), pl.ds(face, face)
    n_near = iter(range(64))
    tail_c = [send(tail_s.at[w], tail_r.at[w], near_sem.at[next(n_near)], s, right) for w in part]
    head_c = [send(head_s.at[w], head_r.at[w], near_sem.at[next(n_near)], s, left) for w in part]
    zd_c = [
        send(zt_s.at[low_rows], zt_r.at[low_rows], near_sem.at[next(n_near)], s, right),
        send(zh_s.at[low_rows], zh_r.at[low_rows], near_sem.at[next(n_near)], s, left),
    ]
    zu_c = [
        send(zt_s.at[high_rows], zt_r.at[high_rows], near_sem.at[next(n_near)], s, right),
        send(zh_s.at[high_rows], zh_r.at[high_rows], near_sem.at[next(n_near)], s, left),
    ]
    below = jnp.maximum(s - 1, 0)
    seed_c = [
        [send(d_s.at[w], d_h.at[0, j], ring_sem.at[0, 0], h, p) for j, p in ((LEFT, right), (RIGHT, left), (OWN, q))]
        for h, w in zip(hosts, part)
    ]
    t_c = [Post(s == h, t_s, t_h.at[below], fed_sem.at[0, below], h, q) for h in hosts]
    a_c = [Post(s == h, a_s.at[w], a_h.at[below], fed_sem.at[1, below], h, q) for h, w in zip(hosts, part)]

    def feed_up(src, dst, kind):
        own = [Post(s == h, x, dst.at[below, 2], fed_sem.at[kind, below], h, q) for h, x in zip(hosts, src)]
        near = [
            [send(x, dst.at[below, j], fed_sem.at[kind, below], h, p) for j, p in ((0, right), (1, left))]
            for h, x in zip(hosts, src)
        ]
        return own, near

    w_own, w_near = feed_up([w_s] * len(hosts), w_h, 2)
    b_own, b_near = feed_up([b_s.at[w] for w in part], b_h, 3)

    def start_up(own, near):
        own.start()

        @pl.when(host)
        def _():
            for c in near:
                c.start()

    group = s // 2
    back_d = [Post(s == t, d_h.at[t - 1, pl.ds(2, 3)], d_home.at[group], home_sem.at[0, group], t, q) for t in range(1, slabs)]
    back_u = [Post(s == t, u_h.at[t - 1, pl.ds(2, 3)], u_home.at[group], home_sem.at[1, group], t, q) for t in range(1, slabs - 1)]
    last_u = send(u0_s, u_home.at[group], home_sem.at[1, group], 0, q)

    def around(buf, n, kind, far):
        near = ((FAR_LEFT, next_right), (FAR_RIGHT, next_left)) if far else ()
        return [
            send(buf.at[n, OWN], buf.at[n, j], ring_sem.at[kind, n], s, p)
            for j, p in ((LEFT, right), (RIGHT, left)) + near
        ]

    round_d = {t: around(d_h, t - 1, 0, t == slabs - 1) for t in range(2, slabs)}
    round_u = {t: around(u_h, t - 1, 1, True) for t in range(1, slabs - 2, 2)}

    count = margin_ref[0, 0]
    row = lax.broadcasted_iota(jnp.int32, (KMAX, KMAX), 0)
    col = lax.broadcasted_iota(jnp.int32, (KMAX, KMAX), 1)
    hit = (row == KMAX - count + col) & (col < count)
    place[...] = jnp.where(hit, 1.0, 0.0).astype(BF)

    loads[0].wait()
    loads[1].wait()
    first = solve(r_v[...].astype(BF), fac, m)
    tail_s[...] = nn(first[-1].astype(BF), place[...]).astype(BF)
    head_s[...] = first[0].astype(BF)

    pl.semaphore_wait(barrier, greeted)

    def send_tails():
        for a, b in zip(tail_c, head_c):
            a.start()
            b.start()

    pl.when(first_slab)(send_tails)

    low = fac[:, :face]
    high = fac[m - face :, m - face :]
    k_tail = jnp.concatenate(
        [tn(low[m - KMAX :], fac[m - KMAX :, m - KMAX :]), tn(high, fac[m - face :, m - KMAX :])], axis=0
    )
    k_head = jnp.concatenate([tn(low, fac[:, :KMAX]), tn(high, fac[m - face :, :KMAX])], axis=0)
    zt_s[...] = nn(k_tail.astype(BF), place[...]).astype(BF)
    zh_s[...] = k_head.astype(BF)

    @pl.when(inner_low)
    def _():
        for c in zd_c:
            c.start()

        pl.when(~host)(send_tails)

    loads[2].wait()
    loads[3].wait()
    for k, piece in enumerate(solve(maps[...], fac, m)):
        gt[:, k * KMAX : (k + 1) * KMAX] = piece.astype(BF)

    @pl.when(~host)
    def _():
        for c in tail_c + head_c:
            c.wait_send()
        pl.semaphore_signal(turn_sem, inc=1, device_id=(pair, q), device_id_type=MESH)

    @pl.when(host)
    def _():
        pl.semaphore_wait(turn_sem, 1)
        send_tails()

    @pl.when(inner_low)
    def _():
        for c in zd_c:
            c.wait_recv()
        zr[low_rows] = nt(zh_r[low_rows], place[...]).astype(BF)
        own = (-gt[:, :face].astype(F32)).T.astype(BF)
        from_left = (0.5 * nt(zt_r[low_rows], gt[:, :KMAX])).astype(BF)
        from_right = (0.5 * nt(zr[low_rows], gt[:, m - KMAX :])).astype(BF)
        for n, block in enumerate((own, from_left, from_right)):
            t_s[n * face : (n + 1) * face, :] = block[:, :face]
            v_s[n * face : (n + 1) * face, :] = block[:, face:]

            @pl.when(~inner_high)
            def _():
                w_s[n * face : (n + 1) * face, :] = block[:, face:]

        @pl.when(inner_high)
        def _():
            for c in t_c:
                c.start()


    def pass_turn():
        pl.semaphore_signal(turn_sem, inc=1, device_id=(pair, q), device_id_type=MESH)

    def tails():
        for g, w in enumerate(part):
            tail_c[g].wait_recv()
            head_c[g].wait_recv()
            adj[w, :] = r_v[w, :]
            adj[w, :KMAX] = adj[w, :KMAX] - 0.5 * tail_r[w].astype(F32)
            adj[w, m - KMAX :] = adj[w, m - KMAX :] - 0.5 * nt(head_r[w], place[...])

            @pl.when(first_slab)
            def _():
                d_s[w] = nt(adj[w, :].astype(BF), gt[:face]).astype(BF)
                for c in seed_c[g]:
                    c.start()

            @pl.when(inner_low)
            def _():
                both = nt(adj[w, :].astype(BF), gt[...]).astype(BF)
                a_s[w] = both[:, :face]
                b_s[w] = both[:, face:]

                @pl.when(inner_high)
                def _():
                    a_c[g].start()

                @pl.when(~inner_high)
                def _():
                    start_up(b_own[g], b_near[g])

    @pl.when(host)
    def _():
        for c in tail_c + head_c:
            c.wait_send()

        @pl.when(inner_high)
        def _():
            for c in zu_c:
                c.start()

        pass_turn()

        @pl.when(~inner_high)
        def _():
            for own_c, near_c in zip(w_own, w_near):
                start_up(own_c, near_c)

    pl.when(s < 3)(tails)

    @pl.when(~host)
    def _():
        pl.when(s > 2)(tails)
        pl.semaphore_wait(turn_sem, 1)
        for c in zu_c:
            c.start()

    def make_up():
        for c in zu_c:
            c.wait_recv()
        zr[high_rows] = nt(zh_r[high_rows], place[...]).astype(BF)

        @pl.when(inner_low)
        def _():
            w_s[:face, :] = (-gt[face:, m - face :].astype(F32)).T.astype(BF)
            w_s[face : 2 * face, :] = (0.5 * nt(zt_r[high_rows], gt[face:, :KMAX])).astype(BF)
            w_s[2 * face :, :] = (0.5 * nt(zr[high_rows], gt[face:, m - KMAX :])).astype(BF)
            for own_c, near_c in zip(w_own, w_near):
                start_up(own_c, near_c)

    def beside(ref, n, slots):
        return jnp.concatenate([ref[n, j] for j in slots], axis=1)

    def take_down(g, w):
        arrived(d_home.at[g], home_sem.at[0, g])

        @pl.when(inner_high)
        def _():
            b_s[w] = (b_s[w].astype(F32) + nn(beside(d_home, g, (2, 0, 1)), v_s[...])).astype(BF)
            start_up(b_own[g], b_near[g])

    def drop_down():
        for g, w in enumerate(part):
            adj[w, :face] = adj[w, :face] - d_home[g, 2].astype(F32)
            adj[w, :KMAX] = adj[w, :KMAX] + 0.5 * nn(d_home[g, 0], zt_r[low_rows])
            adj[w, m - KMAX :] = adj[w, m - KMAX :] + 0.5 * nn(d_home[g, 1], zr[low_rows])

    @pl.when(inner_low & inner_high & ~host)
    def _():
        make_up()
        for g, w in enumerate(part):
            take_down(g, w)

    middle = (OWN, LEFT, RIGHT)

    @pl.when(host)
    def _():
        for t in range(1, slabs - 1):
            n = t - 1
            arrived(t_h.at[n], fed_sem.at[0, n])
            arrived(a_h.at[n], fed_sem.at[1, n])
            slots = d_h.at[n, pl.ds(2, 3 if t == 1 else 2)]
            arrived(slots, ring_sem.at[0, n])
            d_h[n + 1, OWN] = (a_h[n].astype(F32) + nn(beside(d_h, n, middle), t_h[n])).astype(BF)
            for c in round_d[t + 1]:
                c.start()
            back_d[n].start()
            if t == 1:
                pl.when(s > 1)(tails)

            @pl.when(s == t - 1)
            def _():
                make_up()
                for g, w in enumerate(part):
                    take_down(g, w)

        for t in range(slabs - 1, 0, -1):
            n = t - 1
            wide_step = t % 2 == 1
            top = t == slabs - 1
            state = d_h if top else u_h
            arrived(w_h.at[n] if wide_step else w_h.at[n, 2], fed_sem.at[2, n])
            arrived(b_h.at[n] if wide_step else b_h.at[n, 2], fed_sem.at[3, n])
            if wide_step:
                arrived(state.at[n, pl.ds(0, 4)], ring_sem.at[0 if top else 1, n])
            if wide_step:
                around_left, around_right = (LEFT, FAR_LEFT, OWN), (RIGHT, OWN, FAR_RIGHT)
                for j, slots in enumerate((around_left, around_right, middle)):
                    u = (b_h[n, j].astype(F32) + nn(beside(state, n, slots), w_h[n, j])).astype(BF)
                    if t > 1:
                        u_h[n - 1, 2 + j] = u
                    else:
                        u0_s[j] = u
                if t == 1:
                    last_u.start()
            else:
                u_h[n - 1, OWN] = (b_h[n, 2].astype(F32) + nn(beside(state, n, middle), w_h[n, 2])).astype(BF)
                for c in round_u[t - 1]:
                    c.start()
            if top:
                back_d[n].start()
            elif wide_step:
                back_u[n].start()
                back_u[n + 1].start()

    @pl.when(inner_low)
    def _():
        @pl.when(~inner_high)
        def _():
            for g, w in enumerate(part):
                take_down(g, w)

        drop_down()

    @pl.when(first_slab)
    def _():
        make_up()

    @pl.when(inner_high)
    def _():
        for g in range(len(hosts)):
            arrived(u_home.at[g], home_sem.at[1, g])
        for g, w in enumerate(part):
            adj[w, m - face :] = adj[w, m - face :] - u_home[g, 2].astype(F32)
            adj[w, :KMAX] = adj[w, :KMAX] + 0.5 * nn(u_home[g, 0], zt_r[high_rows])
            adj[w, m - KMAX :] = adj[w, m - KMAX :] + 0.5 * nn(u_home[g, 1], zr[high_rows])

    out_ref[...] = halfway(adj[...].astype(BF), fac, m)

    @pl.when(first_slab)
    def _():
        for group_c in seed_c:
            for c in group_c:
                c.wait_send()

    @pl.when(inner_low)
    def _():
        for c in zd_c + b_own + w_own:
            c.wait_send()

    @pl.when(inner_high)
    def _():
        for c in zu_c:
            c.wait_send()

    @pl.when(inner_low & inner_high)
    def _():
        for c in t_c + a_c:
            c.wait_send()

    @pl.when(host)
    def _():
        for c in back_d + back_u + [last_u]:
            c.wait_send()
        for near_c in w_near + b_near + list(round_d.values()) + list(round_u.values()):
            for c in near_c:
                c.wait_send()
    assert names.count <= send_sem.shape[0], names.count


def on_device(slabs, patches, right_side, inverse_factor, forward_trace, backward_trace, margin):
    cols, m = right_side.shape[2:]
    face = forward_trace.shape[2]
    groups = slabs // 2
    rows = cols // groups
    wide = pltpu.VMEM((cols, KMAX), BF)
    square = pltpu.VMEM((2 * face, KMAX), BF)
    thin = pltpu.VMEM((cols, face), BF)
    op = pltpu.VMEM((3 * face, face), BF)
    hbm = pl.BlockSpec(memory_space=pltpu.HBM)
    home = pltpu.VMEM((groups, 3, rows, face), BF)
    fed = pltpu.VMEM((slabs - 1, rows, face), BF)
    fed_up = pltpu.VMEM((slabs - 1, 3, rows, face), BF)
    ops = pltpu.VMEM((slabs - 1, 3 * face, face), BF)
    ops_up = pltpu.VMEM((slabs - 1, 3, 3 * face, face), BF)
    ring = pltpu.VMEM((slabs - 1, 5, rows, face), BF)
    sends = 13 * groups + 6 * slabs - 4
    half = pl.pallas_call(
        functools.partial(kernel, slabs, patches),
        out_shape=pltpu.VMEM((cols, m), BF),
        in_specs=[hbm, hbm, hbm, hbm, pl.BlockSpec(memory_space=pltpu.SMEM)],
        out_specs=pl.BlockSpec(memory_space=pltpu.VMEM),
        scratch_shapes=[
            pltpu.VMEM((cols, m), F32),
            pltpu.VMEM((m, m), BF),
            pltpu.VMEM((2 * face, m), BF),
            wide, wide, square, square, thin, thin, thin, op, op, op,
            wide, wide, square, square, home, home,
            fed, fed_up, ops, ops_up, ring, ring, pltpu.VMEM((3, rows, face), BF),
            pltpu.VMEM((cols, m), F32),
            pltpu.VMEM((2 * face, m), BF),
            pltpu.VMEM((KMAX, KMAX), BF),
            square,
            pltpu.SemaphoreType.DMA((4,)),
            pltpu.SemaphoreType.DMA((sends,)),
            pltpu.SemaphoreType.DMA((2 * groups + 4,)),
            pltpu.SemaphoreType.DMA((2, groups)),
            pltpu.SemaphoreType.DMA((4, slabs - 1)),
            pltpu.SemaphoreType.DMA((2, slabs - 1)),
            pltpu.SemaphoreType.REGULAR,
        ],
        compiler_params=pltpu.CompilerParams(collective_id=0, has_side_effects=True),
        name="sweeps",
    )(right_side, inverse_factor, forward_trace, backward_trace, margin)
    return pl.pallas_call(
        finish,
        out_shape=jax.ShapeDtypeStruct(right_side.shape, F32),
        in_specs=[pl.BlockSpec(memory_space=pltpu.VMEM)] * 2,
        out_specs=hbm,
        scratch_shapes=[pltpu.VMEM((m // KMAX, cols, KMAX), F32), pltpu.SemaphoreType.DMA((m // KMAX,))],
        compiler_params=pltpu.CompilerParams(vmem_limit_bytes=16 << 20),
        name="finish",
    )(half, inverse_factor)


def solution(mesh):
    four = P("slab", "patch", None, None)
    return jax.shard_map(
        functools.partial(on_device, mesh.shape["slab"], mesh.shape["patch"]),
        mesh=mesh,
        in_specs=(four, four, four, four, P("slab", "patch")),
        out_specs=four,
        check_vma=False,
    )
```

time: 41.6 us -> 38.6 us (0.928)
  Pallas kernels: 40.8 us -> 37.4 us
    pallas_call x1, Pallas kernels: 39.5 us -> 36.1 us  [on_device(): pl.pallas_call(functools.partial(kernel, slabs, patches), out_shape=pltpu...]
where the time goes in v2:
time: 38.6 us; the launch traced here: 38.1 us
  Pallas kernels  37.4 us (97%)
  between operations  0.68 us (2%)
    pallas_call x1, Pallas kernels, on_device(): pl.pallas_call(functools.partial(kernel, slabs, patches), out_shape=pltpu...  36.1 us
    pallas_call x1, Pallas kernels, on_device(): pl.pallas_call(finish, out_shape=jax.ShapeDtypeStruct(right_side.shape, F...  1.27 us

profile of v2, /device:TPU:0, one launch (start us, length us, event | category | flops | bytes accessed | tf_op | source)
XLA Modules:
  0.0 38.1 jit_solution(12454308801084165147)
XLA Ops:
  0.7 0.0 copy-start
  0.7 36.1 %sweeps.1.half_ref = bf16[256,768]{1,0:T(8,128)(2,1)S(1)} custom-call(f32[1,1,256,768]{3,2,1,0:T(8,128)} %r_hbm.1, bf16[1,1,768,768]{3,2,1,0:T(8,128)(2,1)} %l_ref.1, bf16[1,1,128,768]{3,2,1,0:T(8,128)(2,1)} %f_hbm.1, bf16[1,1,128,768]{3,2,1,0:T(8,128)(2,1)} %b_hbm.1, s32[1,1]{1,0:T(1,128)S(6)} %copy.6.margin_ref), custom_call_target="tpu_custom_call" | custom-call | tf_op jit(solution)/shard_map/sweeps/pallas_call | solution.py:522
  36.8 0.0 copy-done
  36.8 1.3 %finish.1 = f32[1,1,256,768]{3,2,1,0:T(8,128)} custom-call(bf16[256,768]{1,0:T(8,128)(2,1)S(1)} %sweeps.1.half_ref, bf16[1,1,768,768]{3,2,1,0:T(8,128)(2,1)S(1)} %copy-done), custom_call_target="tpu_custom_call" | custom-call | tf_op jit(solution)/shard_map/finish/pallas_call | solution.py:549
Async XLA Ops:
  0.7 36.1 %copy-start = (bf16[1,1,768,768]{3,2,1,0:T(8,128)(2,1)S(1)}, bf16[1,1,768,768]{3,2,1,0:T(8,128)(2,1)}, u32[]{:S(2)}) copy-start(bf16[1,1,768,768]{3,2,1,0:T(8,128)(2,1)} %l_ref.1) | copy-start | bytes 3538948

commit v3 on v1

v3 whole, which is shorter than its diff:
```python
import functools

import jax
import jax.numpy as jnp
from jax import lax
from jax.experimental import pallas as pl
from jax.experimental.pallas import tpu as pltpu
from jax.sharding import PartitionSpec as P

KMAX = 256
BF = jnp.bfloat16
F32 = jnp.float32
MESH = pl.DeviceIdType.MESH


def nt(a, b):
    return lax.dot_general(a, b, (((1,), (1,)), ((), ())), preferred_element_type=F32)


def nn(a, b):
    return lax.dot_general(a, b, (((1,), (0,)), ((), ())), preferred_element_type=F32)


def tn(a, b):
    return lax.dot_general(a, b, (((0,), (0,)), ((), ())), preferred_element_type=F32)


def halfway(x, fac, m):
    return jnp.concatenate(
        [nt(x[:, : i + KMAX], fac[i : i + KMAX, : i + KMAX]).astype(BF) for i in range(0, m, KMAX)],
        axis=1,
    )


def solve(x, fac, m):
    half = halfway(x, fac, m)
    return [nn(half[:, k:], fac[k:, k : k + KMAX]) for k in range(0, m, KMAX)]


def finish(half_ref, l_ref, out_ref, held, sem):
    m = half_ref.shape[1]
    copies = []
    for n, k in enumerate(range(0, m, KMAX)):
        held[n] = nn(half_ref[:, k:], l_ref[0, 0, k:, k : k + KMAX])
        copies.append(pltpu.make_async_copy(held.at[n], out_ref.at[0, 0, :, k : k + KMAX], sem.at[n]))
        copies[-1].start()
    for c in copies:
        c.wait()


FAR_LEFT, FAR_RIGHT, LEFT, RIGHT, OWN = range(5)
HOST, AIDE = 1, 2


class Names:
    def __init__(self):
        self.count = 0

    def take(self):
        self.count += 1
        return self.count - 1


def kernel(
    slabs, patches, halves,
    r_hbm, l_hbm, f_hbm, b_hbm, margin_ref, out_ref,
    r_v, fac, maps,
    tail_s, head_s, zt_s, zh_s, d_s,
    side_r, z_r, d_home, u_home,
    a_h, b_h, t_h, v_h, w_h, d_h, u_h, u0_s,
    adj, gt, place, zr, lent,
    load_sem, send_sem, near_sem, home_sem, op_sem, term_sem, ring_sem, aide_sem, turn_sem,
):
    s = lax.axis_index("slab")
    q = lax.axis_index("patch")
    left = lax.rem(q + patches - 1, patches)
    right = lax.rem(q + 1, patches)
    next_left = lax.rem(q + patches - 2, patches)
    next_right = lax.rem(q + 2, patches)
    pair = s + 1 - 2 * lax.rem(s, 2)
    odd = lax.rem(s, 2) == 1
    m = fac.shape[-1]
    face = f_hbm.shape[-2]
    cols = r_v.shape[0]
    top = slabs - 1
    wide = cols // halves
    inner_low, inner_high = s > 0, s < top
    first_slab = s == 0
    host, guest, last = s == HOST, s > HOST, s == top
    odd_guest = guest & odd
    aide = s == AIDE

    loads = [
        pltpu.make_async_copy(l_hbm.at[0, 0], fac, load_sem.at[1]),
        pltpu.make_async_copy(r_hbm.at[0, 0], r_v, load_sem.at[0]),
        pltpu.make_async_copy(f_hbm.at[0, 0], maps.at[:face], load_sem.at[2]),
        pltpu.make_async_copy(b_hbm.at[0, 0], maps.at[face:], load_sem.at[3]),
    ]
    for c in loads:
        c.start()

    barrier = pltpu.get_barrier_semaphore()

    def greet(slab, patch):
        pl.semaphore_signal(barrier, inc=1, device_id=(slab, patch), device_id_type=MESH)

    greet(s, left)
    greet(s, right)
    greet(pair, q)

    @pl.when(first_slab)
    def _():
        greet(HOST, left)
        greet(HOST, right)
        greet(AIDE, q)

    @pl.when(aide)
    def _():
        greet(0, q)

    @pl.when(guest)
    def _():
        greet(HOST, q)

    @pl.when(odd_guest)
    def _():
        greet(HOST, left)
        greet(HOST, right)

    @pl.when(host)
    def _():
        greet(s, next_left)
        greet(s, next_right)
        greet(0, left)
        greet(0, right)
        for t in range(HOST + 1, slabs):
            greet(t, q)
        for t in range(HOST + 2, slabs, 2):
            greet(t, left)
            greet(t, right)

    greeted = (
        3
        + first_slab.astype(jnp.int32) * 3
        + aide.astype(jnp.int32)
        + guest.astype(jnp.int32)
        + odd_guest.astype(jnp.int32) * 2
        + host.astype(jnp.int32) * (4 + slabs - 2 + 2 * len(range(HOST + 2, slabs, 2)))
    )

    names = Names()

    class Group:
        def __init__(self, whole, copies):
            self.whole, self.sem = whole, send_sem.at[names.take()]
            self.copies = [
                pltpu.make_async_remote_copy(
                    src_ref=src, dst_ref=dst, send_sem=self.sem, recv_sem=recv, device_id=place, device_id_type=MESH
                )
                for src, dst, recv, place in copies
            ]

        def start(self, first=0, end=None):
            for c in self.copies[first:end]:
                c.start()

        def sent(self):
            arrived(self.whole, self.sem)

    def arrived(ref, sem):
        pltpu.make_async_copy(ref, ref, sem).wait()

    def start(*groups):
        for c in groups:
            c.start()

    def sent(*groups):
        for c in groups:
            c.sent()

    part = [pl.ds(g * wide, wide) for g in range(halves)]
    both = range(halves)
    low_rows, high_rows = pl.ds(0, face), pl.ds(face, face)
    two, four, middle = pl.ds(0, 2), pl.ds(0, 4), pl.ds(2, 3)

    tail_c = [
        Group(
            tail_s,
            [
                (tail_s.at[w], side_r.at[0, w], near_sem.at[g], (s, right)),
                (head_s.at[w], side_r.at[1, w], near_sem.at[g], (s, left)),
            ],
        )
        for g, w in enumerate(part)
    ]

    def z_rows(rows, n):
        return Group(
            zt_s,
            [
                (zt_s.at[rows], z_r.at[0, rows], near_sem.at[halves + n], (s, right)),
                (zh_s.at[rows], z_r.at[1, rows], near_sem.at[halves + n], (s, left)),
            ],
        )

    zd_c, zu_c = z_rows(low_rows, 0), z_rows(high_rows, 1)
    shared = names.count

    seed_c = Group(
        d_h.at[0, :, middle],
        [
            (d_s.at[w], d_h.at[0, g, j], ring_sem.at[g], (HOST, p))
            for g, w in enumerate(part)
            for j, p in ((LEFT, right), (RIGHT, left), (OWN, q))
        ],
    )
    lent_c = Group(
        zt_s,
        [
            (zt_s.at[high_rows], lent.at[0], aide_sem.at[0], (AIDE, q)),
            (zh_s.at[high_rows], lent.at[1], aide_sem.at[0], (AIDE, q)),
        ],
    )
    most = names.count

    names.count = shared
    below = jnp.maximum(s - 1, 0)
    inner = jnp.maximum(s - 2, 0)
    inners = slabs - 3
    sides = ((0, right), (1, left))
    t_sem, v_sem, w_sem = 0, inners, 2 * inners
    a_sem, b_sem, k_sem = 0, halves * inners, halves * inners + slabs - 2
    t_c = Group(t_h.at[below], [(t_h.at[below], t_h.at[below], op_sem.at[t_sem + inner], (HOST, q))])
    v_c = Group(v_h.at[below], [(v_h.at[below], v_h.at[below], op_sem.at[v_sem + inner], (HOST, q))])
    w_to = op_sem.at[w_sem + below]
    w_c = Group(w_h.at[below, 2], [(w_h.at[below, 2], w_h.at[below, 2], w_to, (HOST, q))])
    w_near = Group(w_h.at[below, two], [(w_h.at[below, 2], w_h.at[below, j], w_to, (HOST, p)) for j, p in sides])
    a_c = Group(
        a_h.at[below],
        [(a_h.at[below, g], a_h.at[below, g], term_sem.at[a_sem + halves * inner + g], (HOST, q)) for g in both],
    )
    b_to = term_sem.at[b_sem + inner]
    b_c = Group(b_h.at[below, :, 2], [(b_h.at[below, g, 2], b_h.at[below, g, 2], b_to, (HOST, q)) for g in both])
    b_swap = Group(
        b_h.at[below, :, two],
        [(b_h.at[below, g, 2], b_h.at[below, g, j], near_sem.at[halves + 2], (s, p)) for g in both for j, p in sides],
    )
    b_pass = Group(
        b_h.at[below, :, two],
        [(b_h.at[below, :, two], b_h.at[below, :, two], b_to, (HOST, q))],
    )
    lent_near = Group(
        lent.at[two],
        [
            (lent.at[0], lent.at[2], aide_sem.at[1], (AIDE, right)),
            (lent.at[1], lent.at[3], aide_sem.at[1], (AIDE, left)),
        ],
    )
    lent_back = Group(
        lent.at[two],
        [(lent.at[2 + n], z_r.at[n, high_rows], near_sem.at[halves + 1], (0, q)) for n in range(2)],
    )
    most = max(most, names.count)

    names.count = shared
    close = ((LEFT, right), (RIGHT, left))
    far = close + ((FAR_LEFT, next_right), (FAR_RIGHT, next_left))
    up_rings = range(1, top - 1, 2)

    def ring_of(kind, t):
        return halves * (t - 1) if kind == 0 else halves * (slabs - 1 + up_rings.index(t))

    def around(buf, t, kind, places):
        return Group(
            buf.at[t - 1, :, pl.ds(0, len(places))],
            [
                (buf.at[t - 1, g, OWN], buf.at[t - 1, g, j], ring_sem.at[ring_of(kind, t) + g], (s, p))
                for g in both
                for j, p in places
            ],
        )

    round_d = {t: around(d_h, t, 0, far if t == top else close) for t in range(2, slabs)}
    round_u = {t: around(u_h, t, 1, far) for t in up_rings}
    kept_c = {
        t: Group(
            b_h.at[t - 1, :, two],
            [
                (b_h.at[t - 1, g, 2], b_h.at[t - 1, g, j], term_sem.at[k_sem + t // 2], (s, p))
                for g in both
                for j, p in sides
            ],
        )
        for t in range(1, top, 2)
    }
    w_host = Group(w_h.at[0, two], [(w_h.at[0, 2], w_h.at[0, j], op_sem.at[w_sem], (s, p)) for j, p in sides])

    def back(src, dst, recv, t):
        return Group(src, [(src, dst, recv, (t, q))])

    back_d = {t: back(d_h.at[t - 1, :, middle], d_home, home_sem.at[0], t) for t in range(2, slabs)}
    back_u = {t: back(u_h.at[t - 1, :, middle], u_home, home_sem.at[1], t) for t in range(2, top)}
    last_u = Group(u0_s, [(u0_s.at[g], u_home.at[g], home_sem.at[1 + g], (0, q)) for g in both])
    most = max(most, names.count)
    assert most == send_sem.shape[0], most

    count = margin_ref[0, 0]
    row = lax.broadcasted_iota(jnp.int32, (KMAX, KMAX), 0)
    col = lax.broadcasted_iota(jnp.int32, (KMAX, KMAX), 1)
    hit = (row == KMAX - count + col) & (col < count)
    place[...] = jnp.where(hit, 1.0, 0.0).astype(BF)

    loads[0].wait()
    loads[1].wait()
    first = solve(r_v[...].astype(BF), fac, m)
    tail_s[...] = nn(first[-1].astype(BF), place[...]).astype(BF)
    head_s[...] = first[0].astype(BF)

    pl.semaphore_wait(barrier, greeted)

    def send_tails():
        start(*tail_c)

    pl.when(first_slab)(send_tails)

    low = fac[:, :face]
    high = fac[m - face :, m - face :]
    k_tail = jnp.concatenate(
        [tn(low[m - KMAX :], fac[m - KMAX :, m - KMAX :]), tn(high, fac[m - face :, m - KMAX :])], axis=0
    )
    k_head = jnp.concatenate([tn(low, fac[:, :KMAX]), tn(high, fac[m - face :, :KMAX])], axis=0)
    zt_s[...] = nn(k_tail.astype(BF), place[...]).astype(BF)
    zh_s[...] = k_head.astype(BF)

    @pl.when(inner_low)
    def _():
        start(zd_c)
        pl.when(guest)(send_tails)

    loads[2].wait()
    loads[3].wait()
    for k, piece in enumerate(solve(maps[...], fac, m)):
        gt[:, k * KMAX : (k + 1) * KMAX] = piece.astype(BF)

    @pl.when(first_slab)
    def _():
        tail_c[0].sent()
        pl.semaphore_signal(turn_sem, inc=1, device_id=(HOST, q), device_id_type=MESH)

    @pl.when(host)
    def _():
        pl.semaphore_wait(turn_sem, 1)
        send_tails()

    @pl.when(inner_low)
    def _():
        arrived(z_r.at[:, low_rows], near_sem.at[halves])
        zr[low_rows] = nt(z_r[1, low_rows], place[...]).astype(BF)
        own = (-gt[:, :face].astype(F32)).T.astype(BF)
        from_left = (0.5 * nt(z_r[0, low_rows], gt[:, :KMAX])).astype(BF)
        from_right = (0.5 * nt(zr[low_rows], gt[:, m - KMAX :])).astype(BF)
        for n, block in enumerate((own, from_left, from_right)):
            lines = pl.ds(n * face, face)
            t_h[below, lines] = block[:, :face]

            @pl.when(inner_high)
            def _():
                v_h[below, lines] = block[:, face:]

            @pl.when(~inner_high)
            def _():
                w_h[below, 2, lines] = block[:, face:]

        @pl.when(guest & inner_high)
        def _():
            start(t_c, v_c)

        @pl.when(last)
        def _():
            start(w_c)

    for g, w in enumerate(part):
        arrived(side_r.at[:, w], near_sem.at[g])
        adj[w, :] = r_v[w, :]
        adj[w, :KMAX] = adj[w, :KMAX] - 0.5 * side_r[0, w].astype(F32)
        adj[w, m - KMAX :] = adj[w, m - KMAX :] - 0.5 * nt(side_r[1, w], place[...])

        @pl.when(first_slab)
        def _():
            d_s[w] = nt(adj[w, :].astype(BF), gt[:face]).astype(BF)
            seed_c.start(3 * g, 3 * g + 3)

        @pl.when(inner_low)
        def _():
            terms = nt(adj[w, :].astype(BF), gt[...]).astype(BF)
            a_h[below, g] = terms[:, :face]
            b_h[below, g, 2] = terms[:, face:]

            @pl.when(guest & inner_high)
            def _():
                a_c.start(g, g + 1)

            @pl.when(guest)
            def _():
                b_c.start(g, g + 1)

            @pl.when(last)
            def _():
                b_swap.start(2 * g, 2 * g + 2)

    @pl.when(last)
    def _():
        start(w_near)
        arrived(b_h.at[below, :, two], near_sem.at[halves + 2])
        start(b_pass)

    @pl.when(first_slab)
    def _():
        start(lent_c)

    @pl.when(guest & inner_high)
    def _():
        start(zu_c)

    def make_up():
        arrived(z_r.at[:, high_rows], near_sem.at[halves + 1])
        zr[high_rows] = nt(z_r[1, high_rows], place[...]).astype(BF)

        @pl.when(inner_low)
        def _():
            w_h[below, 2, :face] = (-gt[face:, m - face :].astype(F32)).T.astype(BF)
            w_h[below, 2, face : 2 * face] = (0.5 * nt(z_r[0, high_rows], gt[face:, :KMAX])).astype(BF)
            w_h[below, 2, 2 * face :] = (0.5 * nt(zr[high_rows], gt[face:, m - KMAX :])).astype(BF)

    @pl.when(guest & inner_high)
    def _():
        make_up()
        start(w_c)

        @pl.when(odd)
        def _():
            start(w_near)

    @pl.when(aide)
    def _():
        arrived(lent.at[two], aide_sem.at[0])
        start(lent_near)
        arrived(lent.at[pl.ds(2, 2)], aide_sem.at[1])
        start(lent_back)

    def beside(ref, n, g, slots):
        return jnp.concatenate([ref[n, g, j] for j in slots], axis=1)

    centre = (OWN, LEFT, RIGHT)

    @pl.when(host)
    def _():
        for t in range(1, top):
            n = t - 1
            if t > HOST:
                arrived(t_h.at[n], op_sem.at[t_sem + n - 1])
            for g in both:
                if t > HOST:
                    arrived(a_h.at[n, g], term_sem.at[a_sem + halves * (n - 1) + g])
                arrived(d_h.at[n, g, pl.ds(2, 3 if t == 1 else 2)], ring_sem.at[ring_of(0, t) + g])
                d_h[n + 1, g, OWN] = (a_h[n, g].astype(F32) + nn(beside(d_h, n, g, centre), t_h[n])).astype(BF)
                per = len(far if t + 1 == top else close)
                round_d[t + 1].start(per * g, per * g + per)
            if t == 1:
                start(zu_c)
            if t > HOST:
                back_d[t].start()
                arrived(v_h.at[n], op_sem.at[v_sem + n - 1])
                arrived(b_h.at[n, :, 2], term_sem.at[b_sem + n - 1])
            for g in both:
                b_h[n, g, 2] = (b_h[n, g, 2].astype(F32) + nn(beside(d_h, n, g, centre), v_h[n])).astype(BF)
                if t % 2 == 1:
                    kept_c[t].start(2 * g, 2 * g + 2)
            if t == min(2, top - 1):
                make_up()
                start(w_host)

        arrived(w_h.at[top - 1], op_sem.at[w_sem + top - 1])
        for t in range(top, 0, -2):
            n = t - 1
            state = d_h if t == top else u_h
            if t < top:
                arrived(w_h.at[n, two] if t == HOST else w_h.at[n], op_sem.at[w_sem + n])
            if t > 1:
                arrived(w_h.at[n - 1, 2], op_sem.at[w_sem + n - 1])
            if t == top:
                arrived(b_h.at[n], term_sem.at[b_sem + n - 1])
            else:
                arrived(b_h.at[n, :, two], term_sem.at[k_sem + t // 2])
            for g in both:
                arrived(state.at[n, g, four], ring_sem.at[ring_of(0 if t == top else 1, t) + g])
                for j, slots in enumerate(((LEFT, FAR_LEFT, OWN), (RIGHT, OWN, FAR_RIGHT), centre)):
                    u = (b_h[n, g, j].astype(F32) + nn(beside(state, n, g, slots), w_h[n, j])).astype(BF)
                    if t > 1:
                        u_h[n - 1, g, 2 + j] = u
                    else:
                        u0_s[g, j] = u
                if t > 1:
                    u = b_h[n - 1, g, 2].astype(F32) + nn(beside(u_h, n - 1, g, centre), w_h[n - 1, 2])
                    u_h[n - 2, g, OWN] = u.astype(BF)
                    round_u[t - 2].start(4 * g, 4 * g + 4)
                else:
                    last_u.start(g, g + 1)
            if t == top:
                back_d[t].start()
            elif t > HOST:
                back_u[t].start()
            if t > 1:
                back_u[t - 1].start()

    def drop_low(get):
        for g, w in enumerate(part):
            adj[w, :face] = adj[w, :face] - get(g, 2).astype(F32)
            adj[w, :KMAX] = adj[w, :KMAX] + 0.5 * nn(get(g, 0), z_r[0, low_rows])
            adj[w, m - KMAX :] = adj[w, m - KMAX :] + 0.5 * nn(get(g, 1), zr[low_rows])

    def drop_high(g, get):
        w = part[g]
        adj[w, m - face :] = adj[w, m - face :] - get(g, 2).astype(F32)
        adj[w, :KMAX] = adj[w, :KMAX] + 0.5 * nn(get(g, 0), z_r[0, high_rows])
        adj[w, m - KMAX :] = adj[w, m - KMAX :] + 0.5 * nn(get(g, 1), zr[high_rows])

    @pl.when(host)
    def _():
        drop_low(lambda g, j: d_h[0, g, 2 + j])
        if HOST < top:
            for g in both:
                drop_high(g, lambda g, j: u_h[0, g, 2 + j])

    @pl.when(guest)
    def _():
        arrived(d_home, home_sem.at[0])
        drop_low(lambda g, j: d_home[g, j])

    @pl.when(guest & inner_high)
    def _():
        arrived(u_home, home_sem.at[1])
        for g in both:
            drop_high(g, lambda g, j: u_home[g, j])

    @pl.when(first_slab)
    def _():
        make_up()
        for g in both:
            arrived(u_home.at[g], home_sem.at[1 + g])
            drop_high(g, lambda g, j: u_home[g, j])

    out_ref[...] = halfway(adj[...].astype(BF), fac, m)

    @pl.when(first_slab)
    def _():
        sent(tail_c[1], lent_c, seed_c)

    @pl.when(inner_low)
    def _():
        sent(zd_c, *tail_c)

    @pl.when(inner_low & inner_high)
    def _():
        sent(zu_c)

    @pl.when(aide)
    def _():
        sent(lent_near, lent_back)

    @pl.when(guest)
    def _():
        sent(w_c, b_c)

    @pl.when(guest & inner_high)
    def _():
        sent(t_c, v_c, a_c)

    @pl.when(odd_guest)
    def _():
        sent(w_near)

    @pl.when(last)
    def _():
        sent(b_swap, b_pass)

    @pl.when(host)
    def _():
        sent(w_host, last_u)
        for kind in (round_d, round_u, kept_c, back_d, back_u):
            sent(*kind.values())


def on_device(slabs, patches, right_side, inverse_factor, forward_trace, backward_trace, margin):
    cols, m = right_side.shape[2:]
    face = forward_trace.shape[2]
    halves = 2
    rows = cols // halves
    links = slabs - 1
    wide = pltpu.VMEM((cols, KMAX), BF)
    square = pltpu.VMEM((2 * face, KMAX), BF)
    hbm = pl.BlockSpec(memory_space=pltpu.HBM)
    home = pltpu.VMEM((halves, 3, rows, face), BF)
    ops = pltpu.VMEM((links, 3 * face, face), BF)
    ring = pltpu.VMEM((links, halves, 5, rows, face), BF)
    sends = halves + 2 + max(10, 2 * (links - 1) + (links - 2) + 3 * (slabs // 2 - 1) - (slabs // 2 - 1) + 2)
    half = pl.pallas_call(
        functools.partial(kernel, slabs, patches, halves),
        out_shape=pltpu.VMEM((cols, m), BF),
        in_specs=[hbm, hbm, hbm, hbm, pl.BlockSpec(memory_space=pltpu.SMEM)],
        out_specs=pl.BlockSpec(memory_space=pltpu.VMEM),
        scratch_shapes=[
            pltpu.VMEM((cols, m), F32),
            pltpu.VMEM((m, m), BF),
            pltpu.VMEM((2 * face, m), BF),
            wide, wide, square, square, pltpu.VMEM((cols, face), BF),
            pltpu.VMEM((2, cols, KMAX), BF), pltpu.VMEM((2, 2 * face, KMAX), BF), home, home,
            pltpu.VMEM((links, halves, rows, face), BF),
            pltpu.VMEM((links, halves, 3, rows, face), BF),
            ops, ops, pltpu.VMEM((links, 3, 3 * face, face), BF),
            ring, ring, home,
            pltpu.VMEM((cols, m), F32),
            pltpu.VMEM((2 * face, m), BF),
            pltpu.VMEM((KMAX, KMAX), BF),
            square,
            pltpu.VMEM((4, face, KMAX), BF),
            pltpu.SemaphoreType.DMA((4,)),
            pltpu.SemaphoreType.DMA((sends,)),
            pltpu.SemaphoreType.DMA((halves + 3,)),
            pltpu.SemaphoreType.DMA((1 + halves,)),
            pltpu.SemaphoreType.DMA((2 * (links - 2) + links,)),
            pltpu.SemaphoreType.DMA((halves * (links - 2) + links - 1 + slabs // 2 - 1,)),
            pltpu.SemaphoreType.DMA((halves * (links + slabs // 2 - 1),)),
            pltpu.SemaphoreType.DMA((2,)),
            pltpu.SemaphoreType.REGULAR,
        ],
        compiler_params=pltpu.CompilerParams(collective_id=0, has_side_effects=True),
        name="sweeps",
    )(right_side, inverse_factor, forward_trace, backward_trace, margin)
    return pl.pallas_call(
        finish,
        out_shape=jax.ShapeDtypeStruct(right_side.shape, F32),
        in_specs=[pl.BlockSpec(memory_space=pltpu.VMEM)] * 2,
        out_specs=hbm,
        scratch_shapes=[pltpu.VMEM((m // KMAX, cols, KMAX), F32), pltpu.SemaphoreType.DMA((m // KMAX,))],
        compiler_params=pltpu.CompilerParams(vmem_limit_bytes=16 << 20),
        name="finish",
    )(half, inverse_factor)


def solution(mesh):
    four = P("slab", "patch", None, None)
    return jax.shard_map(
        functools.partial(on_device, mesh.shape["slab"], mesh.shape["patch"]),
        mesh=mesh,
        in_specs=(four, four, four, four, P("slab", "patch")),
        out_specs=four,
        check_vma=False,
    )
```

time: 41.6 us -> 35.2 us (0.85)
  Pallas kernels: 40.8 us -> 34.1 us
    pallas_call x1, Pallas kernels: 39.5 us -> 32.8 us  [on_device(): pl.pallas_call(functools.partial(kernel, slabs, patches, halves), out_sha...]
where the time goes in v3:
time: 35.2 us; the launch traced here: 34.7 us
  Pallas kernels  34.1 us (97%)
  between operations  0.68 us (2%)
    pallas_call x1, Pallas kernels, on_device(): pl.pallas_call(functools.partial(kernel, slabs, patches, halves), out_sha...  32.8 us
    pallas_call x1, Pallas kernels, on_device(): pl.pallas_call(finish, out_shape=jax.ShapeDtypeStruct(right_side.shape, F...  1.27 us

profile of v3, /device:TPU:0, one launch (start us, length us, event | category | flops | bytes accessed | tf_op | source)
XLA Modules:
  0.0 34.7 jit_solution(14783305383863305486)
XLA Ops:
  0.7 0.0 copy-start
  0.7 32.8 %sweeps.1.half_ref = bf16[256,768]{1,0:T(8,128)(2,1)S(1)} custom-call(f32[1,1,256,768]{3,2,1,0:T(8,128)} %r_hbm.1, bf16[1,1,768,768]{3,2,1,0:T(8,128)(2,1)} %l_ref.1, bf16[1,1,128,768]{3,2,1,0:T(8,128)(2,1)} %f_hbm.1, bf16[1,1,128,768]{3,2,1,0:T(8,128)(2,1)} %b_hbm.1, s32[1,1]{1,0:T(1,128)S(6)} %copy.6.margin_ref), custom_call_target="tpu_custom_call" | custom-call | tf_op jit(solution)/shard_map/sweeps/pallas_call | solution.py:607
  33.5 0.0 copy-done
  33.5 1.3 %finish.1 = f32[1,1,256,768]{3,2,1,0:T(8,128)} custom-call(bf16[256,768]{1,0:T(8,128)(2,1)S(1)} %sweeps.1.half_ref, bf16[1,1,768,768]{3,2,1,0:T(8,128)(2,1)S(1)} %copy-done), custom_call_target="tpu_custom_call" | custom-call | tf_op jit(solution)/shard_map/finish/pallas_call | solution.py:640
Async XLA Ops:
  0.7 32.8 %copy-start = (bf16[1,1,768,768]{3,2,1,0:T(8,128)(2,1)S(1)}, bf16[1,1,768,768]{3,2,1,0:T(8,128)(2,1)}, u32[]{:S(2)}) copy-start(bf16[1,1,768,768]{3,2,1,0:T(8,128)(2,1)} %l_ref.1) | copy-start | bytes 3538948

commit v4 on v3

--- a/solution.py
+++ b/solution.py
@@ -295,11 +295,13 @@
     }
     w_host = Group(w_h.at[0, two], [(w_h.at[0, 2], w_h.at[0, j], op_sem.at[w_sem], (s, p)) for j, p in sides])
 
-    def back(src, dst, recv, t):
-        return Group(src, [(src, dst, recv, (t, q))])
-
-    back_d = {t: back(d_h.at[t - 1, :, middle], d_home, home_sem.at[0], t) for t in range(2, slabs)}
-    back_u = {t: back(u_h.at[t - 1, :, middle], u_home, home_sem.at[1], t) for t in range(2, top)}
+    def back(buf, dst, recv, t):
+        return Group(
+            buf.at[t - 1, :, middle], [(buf.at[t - 1, g, middle], dst.at[g], recv, (t, q)) for g in both]
+        )
+
+    back_d = {t: back(d_h, d_home, home_sem.at[0], t) for t in range(2, slabs)}
+    back_u = {t: back(u_h, u_home, home_sem.at[1], t) for t in range(2, top)}
     last_u = Group(u0_s, [(u0_s.at[g], u_home.at[g], home_sem.at[1 + g], (0, q)) for g in both])
     most = max(most, names.count)
     assert most == send_sem.shape[0], most
@@ -335,12 +337,16 @@
     @pl.when(inner_low)
     def _():
         start(zd_c)
-        pl.when(guest)(send_tails)
 
     loads[2].wait()
     loads[3].wait()
     for k, piece in enumerate(solve(maps[...], fac, m)):
         gt[:, k * KMAX : (k + 1) * KMAX] = piece.astype(BF)
+
+    @pl.when(guest)
+    def _():
+        zd_c.sent()
+        send_tails()
 
     @pl.when(first_slab)
     def _():
@@ -399,6 +405,8 @@
             @pl.when(guest & inner_high)
             def _():
                 a_c.start(g, g + 1)
+                if g == 0:
+                    start(zu_c)
 
             @pl.when(guest)
             def _():
@@ -417,10 +425,6 @@
     @pl.when(first_slab)
     def _():
         start(lent_c)
-
-    @pl.when(guest & inner_high)
-    def _():
-        start(zu_c)
 
     def make_up():
         arrived(z_r.at[:, high_rows], near_sem.at[halves + 1])
@@ -470,12 +474,12 @@
                 start(zu_c)
             if t > HOST:
                 back_d[t].start()
+                if t % 2 == 0:
+                    kept_c[t - 1].start()
                 arrived(v_h.at[n], op_sem.at[v_sem + n - 1])
                 arrived(b_h.at[n, :, 2], term_sem.at[b_sem + n - 1])
             for g in both:
                 b_h[n, g, 2] = (b_h[n, g, 2].astype(F32) + nn(beside(d_h, n, g, centre), v_h[n])).astype(BF)
-                if t % 2 == 1:
-                    kept_c[t].start(2 * g, 2 * g + 2)
             if t == min(2, top - 1):
                 make_up()
                 start(w_host)
@@ -504,14 +508,11 @@
                     u = b_h[n - 1, g, 2].astype(F32) + nn(beside(u_h, n - 1, g, centre), w_h[n - 1, 2])
                     u_h[n - 2, g, OWN] = u.astype(BF)
                     round_u[t - 2].start(4 * g, 4 * g + 4)
+                    back_u[t - 1].start(g, g + 1)
                 else:
                     last_u.start(g, g + 1)
-            if t == top:
-                back_d[t].start()
-            elif t > HOST:
-                back_u[t].start()
-            if t > 1:
-                back_u[t - 1].start()
+                if t > HOST:
+                    (back_d if t == top else back_u)[t].start(g, g + 1)
 
     def drop_low(get):
         for g, w in enumerate(part):
@@ -550,7 +551,8 @@
             arrived(u_home.at[g], home_sem.at[1 + g])
             drop_high(g, lambda g, j: u_home[g, j])
 
-    out_ref[...] = halfway(adj[...].astype(BF), fac, m)
+    for k, piece in enumerate(solve(adj[...].astype(BF), fac, m)):
+        out_ref[0, 0, :, k * KMAX : (k + 1) * KMAX] = piece
 
     @pl.when(first_slab)
     def _():
@@ -558,7 +560,15 @@
 
     @pl.when(inner_low)
     def _():
-        sent(zd_c, *tail_c)
+        sent(tail_c[1])
+
+    @pl.when(host)
+    def _():
+        sent(zd_c, tail_c[0])
+
+    @pl.when(guest)
+    def _():
+        sent(tail_c[0])
 
     @pl.when(inner_low & inner_high)
     def _():
@@ -604,9 +614,9 @@
     ops = pltpu.VMEM((links, 3 * face, face), BF)
     ring = pltpu.VMEM((links, halves, 5, rows, face), BF)
     sends = halves + 2 + max(10, 2 * (links - 1) + (links - 2) + 3 * (slabs // 2 - 1) - (slabs // 2 - 1) + 2)
-    half = pl.pallas_call(
+    return pl.pallas_call(
         functools.partial(kernel, slabs, patches, halves),
-        out_shape=pltpu.VMEM((cols, m), BF),
+        out_shape=pltpu.VMEM(right_side.shape, F32),
         in_specs=[hbm, hbm, hbm, hbm, pl.BlockSpec(memory_space=pltpu.SMEM)],
         out_specs=pl.BlockSpec(memory_space=pltpu.VMEM),
         scratch_shapes=[

time: 35.2 us -> 33.9 us (0.963)
  Pallas kernels: 34.1 us -> 32.2 us
  local copies, waits for them, and re-layouts: 0.01 us -> 0.88 us
    pallas_call x1 -> x0, Pallas kernels: 1.27 us -> none  [on_device(): pl.pallas_call(finish, out_shape=jax.ShapeDtypeStruct(right_side.shape, F...]
    unnamed x2 -> x1, local copies, waits for them, and re-layouts: 0.01 us -> 0.88 us
    pallas_call x1, Pallas kernels: 32.8 us -> 32.2 us  [on_device(): pl.pallas_call(functools.partial(kernel, slabs, patches, halves), out_sha...]
where the time goes in v4:
time: 33.9 us; the launch traced here: 33.7 us
  Pallas kernels  32.2 us (95%)
  local copies, waits for them, and re-layouts  0.88 us (3%)
  between operations  0.66 us (2%)
    pallas_call x1, Pallas kernels, on_device(): pl.pallas_call(functools.partial(kernel, slabs, patches, halves), out_sha...  32.2 us
    unnamed x1, local copies, waits for them, and re-layouts  0.88 us

profile of v4, /device:TPU:0, one launch (start us, length us, event | category | flops | bytes accessed | tf_op | source)
XLA Modules:
  0.0 33.7 jit_solution(2014760513337621239)
XLA Ops:
  0.7 32.2 %sweeps.1 = f32[1,1,256,768]{3,2,1,0:T(8,128)S(1)} custom-call(f32[1,1,256,768]{3,2,1,0:T(8,128)} %r_hbm.1, bf16[1,1,768,768]{3,2,1,0:T(8,128)(2,1)} %l_hbm.1, bf16[1,1,128,768]{3,2,1,0:T(8,128)(2,1)} %f_hbm.1, bf16[1,1,128,768]{3,2,1,0:T(8,128)(2,1)} %b_hbm.1, s32[1,1]{1,0:T(1,128)S(6)} %copy.8.margin_ref), custom_call_target="tpu_custom_call" | custom-call | tf_op jit(solution)/shard_map/sweeps/pallas_call | solution.py:617
  32.8 0.9 %copy.7 = f32[1,1,256,768]{3,2,1,0:T(8,128)} copy(f32[1,1,256,768]{3,2,1,0:T(8,128)S(1)} %sweeps.1) | data formatting | bytes 1572864

commit v5 on v4

--- a/solution.py
+++ b/solution.py
@@ -68,7 +68,7 @@
     tail_s, head_s, zt_s, zh_s, d_s,
     side_r, z_r, d_home, u_home,
     a_h, b_h, t_h, v_h, w_h, d_h, u_h, u0_s,
-    adj, gt, place, zr, lent,
+    adj, gt, place, zr, lent, effect,
     load_sem, send_sem, near_sem, home_sem, op_sem, term_sem, ring_sem, aide_sem, turn_sem,
 ):
     s = lax.axis_index("slab")
@@ -253,7 +253,7 @@
         lent.at[two],
         [
             (lent.at[0], lent.at[2], aide_sem.at[1], (AIDE, right)),
-            (lent.at[1], lent.at[3], aide_sem.at[1], (AIDE, left)),
+            (lent.at[1], lent.at[3], aide_sem.at[2], (AIDE, left)),
         ],
     )
     lent_back = Group(
@@ -334,9 +334,31 @@
     zt_s[...] = nn(k_tail.astype(BF), place[...]).astype(BF)
     zh_s[...] = k_head.astype(BF)
 
+    far_right, far_left = q == patches - 1, q == 0
+
+    def lift_far():
+        @pl.when(far_right)
+        def _():
+            zu_c.start(0, 1)
+
+        @pl.when(far_left)
+        def _():
+            zu_c.start(1, 2)
+
+    def lift():
+        @pl.when(~far_right)
+        def _():
+            zu_c.start(0, 1)
+
+        @pl.when(~far_left)
+        def _():
+            zu_c.start(1, 2)
+
     @pl.when(inner_low)
     def _():
         start(zd_c)
+
+    pl.when(guest & inner_high)(lift_far)
 
     loads[2].wait()
     loads[3].wait()
@@ -406,7 +428,7 @@
             def _():
                 a_c.start(g, g + 1)
                 if g == 0:
-                    start(zu_c)
+                    lift()
 
             @pl.when(guest)
             def _():
@@ -425,6 +447,9 @@
     @pl.when(first_slab)
     def _():
         start(lent_c)
+        for k, piece in enumerate(solve(adj[...].astype(BF), fac, m)):
+            out_ref[0, 0, :, k * KMAX : (k + 1) * KMAX] = piece
+        effect[:face] = (-tn(fac[m - face :, m - face :], fac[m - face :, :])).astype(BF)
 
     def make_up():
         arrived(z_r.at[:, high_rows], near_sem.at[halves + 1])
@@ -449,13 +474,37 @@
     def _():
         arrived(lent.at[two], aide_sem.at[0])
         start(lent_near)
-        arrived(lent.at[pl.ds(2, 2)], aide_sem.at[1])
-        start(lent_back)
+
+        @pl.when(q == 0)
+        def _():
+            arrived(lent.at[3], aide_sem.at[2])
+            lent_back.start(1, 2)
+            arrived(lent.at[2], aide_sem.at[1])
+            lent_back.start(0, 1)
+
+        @pl.when(q > 0)
+        def _():
+            arrived(lent.at[2], aide_sem.at[1])
+            lent_back.start(0, 1)
+            arrived(lent.at[3], aide_sem.at[2])
+            lent_back.start(1, 2)
 
     def beside(ref, n, g, slots):
         return jnp.concatenate([ref[n, g, j] for j in slots], axis=1)
 
     centre = (OWN, LEFT, RIGHT)
+
+    def drop_low(get):
+        for g, w in enumerate(part):
+            adj[w, :face] = adj[w, :face] - get(g, 2).astype(F32)
+            adj[w, :KMAX] = adj[w, :KMAX] + 0.5 * nn(get(g, 0), z_r[0, low_rows])
+            adj[w, m - KMAX :] = adj[w, m - KMAX :] + 0.5 * nn(get(g, 1), zr[low_rows])
+
+    def drop_high(g, get):
+        w = part[g]
+        adj[w, m - face :] = adj[w, m - face :] - get(g, 2).astype(F32)
+        adj[w, :KMAX] = adj[w, :KMAX] + 0.5 * nn(get(g, 0), z_r[0, high_rows])
+        adj[w, m - KMAX :] = adj[w, m - KMAX :] + 0.5 * nn(get(g, 1), zr[high_rows])
 
     @pl.when(host)
     def _():
@@ -484,6 +533,7 @@
                 make_up()
                 start(w_host)
 
+        drop_low(lambda g, j: d_h[0, g, 2 + j])
         arrived(w_h.at[top - 1], op_sem.at[w_sem + top - 1])
         for t in range(top, 0, -2):
             n = t - 1
@@ -514,21 +564,8 @@
                 if t > HOST:
                     (back_d if t == top else back_u)[t].start(g, g + 1)
 
-    def drop_low(get):
-        for g, w in enumerate(part):
-            adj[w, :face] = adj[w, :face] - get(g, 2).astype(F32)
-            adj[w, :KMAX] = adj[w, :KMAX] + 0.5 * nn(get(g, 0), z_r[0, low_rows])
-            adj[w, m - KMAX :] = adj[w, m - KMAX :] + 0.5 * nn(get(g, 1), zr[low_rows])
-
-    def drop_high(g, get):
-        w = part[g]
-        adj[w, m - face :] = adj[w, m - face :] - get(g, 2).astype(F32)
-        adj[w, :KMAX] = adj[w, :KMAX] + 0.5 * nn(get(g, 0), z_r[0, high_rows])
-        adj[w, m - KMAX :] = adj[w, m - KMAX :] + 0.5 * nn(get(g, 1), zr[high_rows])
-
     @pl.when(host)
     def _():
-        drop_low(lambda g, j: d_h[0, g, 2 + j])
         if HOST < top:
             for g in both:
                 drop_high(g, lambda g, j: u_h[0, g, 2 + j])
@@ -546,13 +583,25 @@
 
     @pl.when(first_slab)
     def _():
-        make_up()
-        for g in both:
+        arrived(z_r.at[:, high_rows], near_sem.at[halves + 1])
+        half = jnp.concatenate(
+            [nt(z_r[0, high_rows], fac[i : i + KMAX, :KMAX]).astype(BF) for i in range(0, m, KMAX)], axis=1
+        )
+        for k in range(0, m, KMAX):
+            spread = 0.5 * nn(half[:, k:], fac[k:, k : k + KMAX])
+            effect[face : 2 * face, k : k + KMAX] = spread.astype(BF)
+        at_tail = nt(z_r[1, high_rows], place[...]).astype(BF)
+        half = nt(at_tail, fac[m - KMAX :, m - KMAX :]).astype(BF)
+        effect[2 * face :] = (0.5 * nn(half, fac[m - KMAX :, :])).astype(BF)
+        for g, w in enumerate(part):
             arrived(u_home.at[g], home_sem.at[1 + g])
-            drop_high(g, lambda g, j: u_home[g, j])
-
-    for k, piece in enumerate(solve(adj[...].astype(BF), fac, m)):
-        out_ref[0, 0, :, k * KMAX : (k + 1) * KMAX] = piece
+            u = jnp.concatenate([u_home[g, j] for j in (2, 0, 1)], axis=1)
+            out_ref[0, 0, w, :] = out_ref[0, 0, w, :] + nn(u, effect[...])
+
+    @pl.when(inner_low)
+    def _():
+        for k, piece in enumerate(solve(adj[...].astype(BF), fac, m)):
+            out_ref[0, 0, :, k * KMAX : (k + 1) * KMAX] = piece
 
     @pl.when(first_slab)
     def _():
@@ -634,6 +683,7 @@
             pltpu.VMEM((KMAX, KMAX), BF),
             square,
             pltpu.VMEM((4, face, KMAX), BF),
+            pltpu.VMEM((3 * face, m), BF),
             pltpu.SemaphoreType.DMA((4,)),
             pltpu.SemaphoreType.DMA((sends,)),
             pltpu.SemaphoreType.DMA((halves + 3,)),
@@ -641,7 +691,7 @@
             pltpu.SemaphoreType.DMA((2 * (links - 2) + links,)),
             pltpu.SemaphoreType.DMA((halves * (links - 2) + links - 1 + slabs // 2 - 1,)),
             pltpu.SemaphoreType.DMA((halves * (links + slabs // 2 - 1),)),
-            pltpu.SemaphoreType.DMA((2,)),
+            pltpu.SemaphoreType.DMA((3,)),
             pltpu.SemaphoreType.REGULAR,
         ],
         compiler_params=pltpu.CompilerParams(collective_id=0, has_side_effects=True),

time: 33.9 us -> 33.1 us (0.976)
  Pallas kernels: 32.2 us -> 31.4 us
    pallas_call x1, Pallas kernels: 32.2 us -> 31.4 us  [on_device(): pl.pallas_call(functools.partial(kernel, slabs, patches, halves), out_sha...]
where the time goes in v5:
time: 33.1 us; the launch traced here: 32.9 us
  Pallas kernels  31.4 us (95%)
  local copies, waits for them, and re-layouts  0.88 us (3%)
  between operations  0.66 us (2%)
    pallas_call x1, Pallas kernels, on_device(): pl.pallas_call(functools.partial(kernel, slabs, patches, halves), out_sha...  31.4 us
    unnamed x1, local copies, waits for them, and re-layouts  0.88 us

profile of v5, /device:TPU:0, one launch (start us, length us, event | category | flops | bytes accessed | tf_op | source)
XLA Modules:
  0.0 32.9 jit_solution(3703008785788655763)
XLA Ops:
  0.7 31.4 %sweeps.1 = f32[1,1,256,768]{3,2,1,0:T(8,128)S(1)} custom-call(f32[1,1,256,768]{3,2,1,0:T(8,128)} %r_hbm.1, bf16[1,1,768,768]{3,2,1,0:T(8,128)(2,1)} %l_hbm.1, bf16[1,1,128,768]{3,2,1,0:T(8,128)(2,1)} %f_hbm.1, bf16[1,1,128,768]{3,2,1,0:T(8,128)(2,1)} %b_hbm.1, s32[1,1]{1,0:T(1,128)S(6)} %copy.8.margin_ref), custom_call_target="tpu_custom_call" | custom-call | tf_op jit(solution)/shard_map/sweeps/pallas_call | solution.py:666
  32.1 0.9 %copy.7 = f32[1,1,256,768]{3,2,1,0:T(8,128)} copy(f32[1,1,256,768]{3,2,1,0:T(8,128)S(1)} %sweeps.1) | data formatting | bytes 1572864

commit v6 on v5

--- a/solution.py
+++ b/solution.py
@@ -90,15 +90,16 @@
     odd_guest = guest & odd
     aide = s == AIDE
 
-    loads = [
-        pltpu.make_async_copy(l_hbm.at[0, 0], fac, load_sem.at[1]),
-        pltpu.make_async_copy(r_hbm.at[0, 0], r_v, load_sem.at[0]),
-        pltpu.make_async_copy(f_hbm.at[0, 0], maps.at[:face], load_sem.at[2]),
-        pltpu.make_async_copy(b_hbm.at[0, 0], maps.at[face:], load_sem.at[3]),
+    steps = range(0, m, KMAX)
+    r_load = pltpu.make_async_copy(r_hbm.at[0, 0], r_v, load_sem.at[0])
+    l_loads = []
+    for n, i in enumerate(steps):
+        block = (pl.ds(i, KMAX), pl.ds(0, i + KMAX))
+        l_loads.append(pltpu.make_async_copy(l_hbm.at[(0, 0, *block)], fac.at[block], load_sem.at[1 + n]))
+    map_loads = [
+        pltpu.make_async_copy(f_hbm.at[0, 0], maps.at[:face], load_sem.at[0]),
+        pltpu.make_async_copy(b_hbm.at[0, 0], maps.at[face:], load_sem.at[0]),
     ]
-    for c in loads:
-        c.start()
-
     barrier = pltpu.get_barrier_semaphore()
 
     def greet(slab, patch):
@@ -138,6 +139,10 @@
         for t in range(HOST + 2, slabs, 2):
             greet(t, left)
             greet(t, right)
+
+    r_load.start()
+    for c in l_loads:
+        c.start()
 
     greeted = (
         3
@@ -312,11 +317,15 @@
     hit = (row == KMAX - count + col) & (col < count)
     place[...] = jnp.where(hit, 1.0, 0.0).astype(BF)
 
-    loads[0].wait()
-    loads[1].wait()
-    first = solve(r_v[...].astype(BF), fac, m)
-    tail_s[...] = nn(first[-1].astype(BF), place[...]).astype(BF)
-    head_s[...] = first[0].astype(BF)
+    r_load.wait()
+    for c in l_loads:
+        c.wait()
+    for c in map_loads:
+        c.start()
+    half = halfway(r_v[...].astype(BF), fac, m)
+    at_tail = nn(half[:, m - KMAX :], fac[m - KMAX :, m - KMAX :]).astype(BF)
+    tail_s[...] = nn(at_tail, place[...]).astype(BF)
+    head_s[...] = nn(half, fac[:, :KMAX]).astype(BF)
 
     pl.semaphore_wait(barrier, greeted)
 
@@ -360,8 +369,7 @@
 
     pl.when(guest & inner_high)(lift_far)
 
-    loads[2].wait()
-    loads[3].wait()
+    arrived(maps, load_sem.at[0])
     for k, piece in enumerate(solve(maps[...], fac, m)):
         gt[:, k * KMAX : (k + 1) * KMAX] = piece.astype(BF)
 
@@ -684,7 +692,7 @@
             square,
             pltpu.VMEM((4, face, KMAX), BF),
             pltpu.VMEM((3 * face, m), BF),
-            pltpu.SemaphoreType.DMA((4,)),
+            pltpu.SemaphoreType.DMA((2 + m // KMAX,)),
             pltpu.SemaphoreType.DMA((sends,)),
             pltpu.SemaphoreType.DMA((halves + 3,)),
             pltpu.SemaphoreType.DMA((1 + halves,)),

time: 33.1 us -> 33.1 us (level)
  no operation moved by 1% of the time
where the time goes in v6:
time: 33.1 us; the launch traced here: 33 us
  Pallas kernels  31.5 us (95%)
  local copies, waits for them, and re-layouts  0.88 us (3%)
  between operations  0.66 us (2%)
    pallas_call x1, Pallas kernels, on_device(): pl.pallas_call(functools.partial(kernel, slabs, patches, halves), out_sha...  31.5 us
    unnamed x1, local copies, waits for them, and re-layouts  0.88 us

profile of v6, /device:TPU:0, one launch (start us, length us, event | category | flops | bytes accessed | tf_op | source)
XLA Modules:
  0.0 33.0 jit_solution(12618898713512274383)
XLA Ops:
  0.7 31.5 %sweeps.1 = f32[1,1,256,768]{3,2,1,0:T(8,128)S(1)} custom-call(f32[1,1,256,768]{3,2,1,0:T(8,128)} %r_hbm.1, bf16[1,1,768,768]{3,2,1,0:T(8,128)(2,1)} %l_hbm.1, bf16[1,1,128,768]{3,2,1,0:T(8,128)(2,1)} %f_hbm.1, bf16[1,1,128,768]{3,2,1,0:T(8,128)(2,1)} %b_hbm.1, s32[1,1]{1,0:T(1,128)S(6)} %copy.8.margin_ref), custom_call_target="tpu_custom_call" | custom-call | tf_op jit(solution)/shard_map/sweeps/pallas_call | solution.py:674
  32.1 0.9 %copy.7 = f32[1,1,256,768]{3,2,1,0:T(8,128)} copy(f32[1,1,256,768]{3,2,1,0:T(8,128)S(1)} %sweeps.1) | data formatting | bytes 1572864

commit v7 on v6

--- a/solution.py
+++ b/solution.py
@@ -332,7 +332,9 @@
     def send_tails():
         start(*tail_c)
 
-    pl.when(first_slab)(send_tails)
+    @pl.when(first_slab)
+    def _():
+        tail_c[0].start()
 
     low = fac[:, :face]
     high = fac[m - face :, m - face :]
@@ -342,6 +344,10 @@
     k_head = jnp.concatenate([tn(low, fac[:, :KMAX]), tn(high, fac[m - face :, :KMAX])], axis=0)
     zt_s[...] = nn(k_tail.astype(BF), place[...]).astype(BF)
     zh_s[...] = k_head.astype(BF)
+
+    @pl.when(first_slab)
+    def _():
+        tail_c[1].start()
 
     far_right, far_left = q == patches - 1, q == 0
 
@@ -445,10 +451,11 @@
             @pl.when(last)
             def _():
                 b_swap.start(2 * g, 2 * g + 2)
+                if g == 0:
+                    start(w_near)
 
     @pl.when(last)
     def _():
-        start(w_near)
         arrived(b_h.at[below, :, two], near_sem.at[halves + 2])
         start(b_pass)
 

time: 33.1 us -> 33.2 us (level)
  no operation moved by 1% of the time
where the time goes in v7:
time: 33.2 us; the launch traced here: 33 us
  Pallas kernels  31.5 us (95%)
  local copies, waits for them, and re-layouts  0.88 us (3%)
  between operations  0.66 us (2%)
    pallas_call x1, Pallas kernels, on_device(): pl.pallas_call(functools.partial(kernel, slabs, patches, halves), out_sha...  31.5 us
    unnamed x1, local copies, waits for them, and re-layouts  0.88 us

profile of v7, /device:TPU:0, one launch (start us, length us, event | category | flops | bytes accessed | tf_op | source)
XLA Modules:
  0.0 33.0 jit_solution(4642151429193258702)
XLA Ops:
  0.7 31.5 %sweeps.1 = f32[1,1,256,768]{3,2,1,0:T(8,128)S(1)} custom-call(f32[1,1,256,768]{3,2,1,0:T(8,128)} %r_hbm.1, bf16[1,1,768,768]{3,2,1,0:T(8,128)(2,1)} %l_hbm.1, bf16[1,1,128,768]{3,2,1,0:T(8,128)(2,1)} %f_hbm.1, bf16[1,1,128,768]{3,2,1,0:T(8,128)(2,1)} %b_hbm.1, s32[1,1]{1,0:T(1,128)S(6)} %copy.8.margin_ref), custom_call_target="tpu_custom_call" | custom-call | tf_op jit(solution)/shard_map/sweeps/pallas_call | solution.py:681
  32.1 0.9 %copy.7 = f32[1,1,256,768]{3,2,1,0:T(8,128)} copy(f32[1,1,256,768]{3,2,1,0:T(8,128)S(1)} %sweeps.1) | data formatting | bytes 1572864
